TPU v7x, 32 devices: a whole 2x2x4 slice. The times are simulated.
32 devices in a mesh: gx: 4 (over z), gy: 8 (over y, x, core).
Axes of the slice: x: 2, y: 2, z: 4, core: 2. Of those that a mesh axis runs over, the one named last changes fastest.
Arguments:
- state_prev: float32 [128, 128, 512], P('gy', None, 'gx'), may hold values from -60 to 60
- diffusivity: float32 [128, 128, 512], P('gy', None, 'gx'), may hold values from 0.5 to 4
- vapour: float32 [128, 128, 512], P('gy', None, 'gx'), may hold values from 0.01 to 0.1
- cos_zenith: float32 [128, 512], P('gy', 'gx'), may hold values from 0.1 to 1
- albedo: float32 [128, 512], P('gy', 'gx'), may hold values from 0.05 to 0.8
- absorption: float32 [128, 112], replicated, may hold values from 0.005 to 1
- solar_weight: float32 [112], replicated, may hold values from 0.002 to 0.02
- day_mask: int32 [512], P(('gx', 'gy')), may hold values from 0 to 1, as said below
Outputs:
- state_next: float32 [128, 128, 512], P('gy', None, 'gx')
- residual: float32 [128, 128, 512], P('gy', None, 'gx')
- net_flux: float32 [128, 128, 512], P('gy', None, 'gx')
Inputs may be any that keep to these rules, and one draw needn't show every extreme that they name: `day_mask`: exactly half of the 512 entries are 1, and some device holds only sunlit blocks.
All inputs are finite; a program needn't handle non-finite values.
Results may differ from a plain program's by a relative error of at most 0.00015.
Values sent between devices are 32-bit elements; how exact they have to be, the bound alone decides.
A program may use at most 128 MiB of HBM per device.

v0:
```python
import jax
import jax.numpy as jnp
from jax import lax
from jax.sharding import PartitionSpec as P

ITERS = 5


def padded(array, sides, width, wrap):
    for axis, dim in sides:
        devices, length = (lax.axis_size(axis), array.shape[dim])
        up = [(i, (i + 1) % devices) for i in range(devices if wrap else devices - 1)]
        down = [(j, i) for i, j in up]
        last = lax.slice_in_dim(array, length - width, length, axis=dim)
        first = lax.slice_in_dim(array, 0, width, axis=dim)
        before = lax.ppermute(last, axis, up)
        after = lax.ppermute(first, axis, down)
        array = jnp.concatenate([before, array, after], axis=dim)
    return array


def longitude_edges(values):
    return padded(values, (("gx", 2),), 1, True)


def latitude_edges(values):
    return padded(values, (("gy", 0),), 1, False)


def face_terms(diffusivity):
    widened = longitude_edges(diffusivity)
    extended = latitude_edges(diffusivity)
    east_face = jnp.sqrt(diffusivity * widened[:, :, 2:])
    west_face = jnp.sqrt(diffusivity * widened[:, :, :-2])
    north_face = jnp.sqrt(diffusivity * extended[2:])
    south_face = jnp.sqrt(diffusivity * extended[:-2])
    level_face = jnp.sqrt(diffusivity[:, 1:] * diffusivity[:, :-1])
    return (east_face, west_face, north_face, south_face, level_face)


def operate(values, conductances):
    east_face, west_face, north_face, south_face, level_face = conductances
    widened = longitude_edges(values)
    extended = latitude_edges(values)
    applied = (
        values
        + east_face * (values - widened[:, :, 2:])
        + west_face * (values - widened[:, :, :-2])
    )
    applied = applied + north_face * (values - extended[2:]) + south_face * (values - extended[:-2])
    vertical = level_face * (values[:, 1:] - values[:, :-1])
    padding = jnp.zeros_like(values[:, :1])
    return (
        applied - jnp.concatenate([vertical, padding], 1) + jnp.concatenate([padding, vertical], 1)
    )


def squares(residual):
    return lax.psum(jnp.sum(residual * residual), ("gx", "gy"))


def radiate(layer_amount, sunlight, triangle, absorption, solar_weight):
    levels = layer_amount.shape[0]
    columns = layer_amount.shape[1]
    gpoints = absorption.shape[1]
    thickness = absorption[:, :, None] * layer_amount[:, None, :]
    cumulative = jnp.dot(
        triangle,
        thickness.reshape(levels, gpoints * columns),
        precision=lax.Precision.HIGHEST,
        preferred_element_type=jnp.float32,
    )
    cumulative = cumulative.reshape(levels, gpoints, columns)
    cosine = sunlight[0]
    surface = sunlight[1]
    downward = cosine * jnp.exp(-cumulative / cosine)
    upward = surface * downward[-1] * jnp.exp(-1.66 * (cumulative[-1] - cumulative))
    return jnp.einsum("lgc,g->lc", downward - upward, solar_weight, precision=lax.Precision.HIGHEST)


def body(state_prev, diffusivity, vapour, cos_zenith, albedo, absorption, solar_weight, day_mask):
    conductances = face_terms(diffusivity)
    state_next = state_prev
    residual = state_prev - operate(state_prev, conductances)
    direction = residual
    current = squares(residual)
    for iteration in range(ITERS):
        applied = operate(direction, conductances)
        curvature_sum = lax.psum(jnp.sum(direction * applied), ("gx", "gy"))
        step_size = current / curvature_sum
        state_next = state_next + step_size * direction
        residual = residual - step_size * applied
        following = squares(residual)
        direction = residual + following / current * direction
        current = following
    optical = vapour * (1.0 + 0.5 * jnp.tanh(state_prev))
    sunlight = jnp.stack([cos_zenith, albedo], 1)
    levels = optical.shape[1]
    triangle = (
        lax.broadcasted_iota(jnp.int32, (levels, levels), 0)
        >= lax.broadcasted_iota(jnp.int32, (levels, levels), 1)
    ).astype(jnp.float32)

    def slab_flux(inputs):
        return radiate(inputs[0], inputs[1], triangle, absorption, solar_weight)

    lit_blocks = day_mask.astype(jnp.float32)[:, None, None]
    whole_mask = lax.all_gather(day_mask, ("gx", "gy"), axis=0, tiled=True)
    devices = lax.axis_size("gx") * lax.axis_size("gy")
    blocks = day_mask.shape[0]
    width = optical.shape[2]
    capacity = blocks * width // devices
    working = blocks * width // 2
    myself = lax.axis_index("gx") * lax.axis_size("gy") + lax.axis_index("gy")
    per_device = jnp.sum(whole_mask.reshape(devices, blocks), 1)
    ends = jnp.cumsum(per_device) * width
    starts = ends - per_device * width
    my_start = jnp.take(starts, myself)
    my_end = jnp.take(ends, myself)
    own_rank = jnp.cumsum(day_mask) - 1
    peer_ids = lax.broadcasted_iota(jnp.int32, (devices, capacity), 0)
    slot_ids = lax.broadcasted_iota(jnp.int32, (devices, capacity), 1)
    first = my_start + (peer_ids - my_start) % devices
    wanted = first + slot_ids * devices
    valid_send = (wanted < my_end).astype(jnp.float32)
    offset = wanted - my_start
    rank_needed = offset // width
    row_hits = (own_rank[None, None, :] == rank_needed[:, :, None]) & (day_mask[None, None, :] == 1)
    row_ids = lax.broadcasted_iota(jnp.int32, (1, 1, blocks), 2)
    row_of = jnp.sum(jnp.where(row_hits, row_ids, 0), 2)
    flat_send = jnp.clip(row_of * width + offset % width, 0, blocks * width - 1)
    packed = jnp.concatenate([optical, sunlight], 1)
    packed = jnp.transpose(packed, (1, 0, 2)).reshape(levels + 2, blocks * width)
    outgoing = jnp.take(packed, flat_send.reshape(-1), 1).reshape(levels + 2, devices, capacity)
    outgoing = jnp.transpose(outgoing * valid_send[None], (1, 0, 2))
    arrived = lax.all_to_all(outgoing, ("gx", "gy"), split_axis=0, concat_axis=0, tiled=True)
    work_ids = lax.broadcasted_iota(jnp.int32, (working,), 0)
    global_ids = work_ids * devices + myself
    source = jnp.sum((ends[None, :] <= global_ids[:, None]).astype(jnp.int32), 1)
    source = jnp.clip(source, 0, devices - 1)
    source_start = jnp.take(starts, source)
    source_first = source_start + (myself - source_start) % devices
    flat_work = jnp.clip(
        source * capacity + (global_ids - source_first) // devices, 0, devices * capacity - 1
    )
    arrived_flat = jnp.transpose(arrived, (1, 0, 2)).reshape(levels + 2, devices * capacity)
    work = jnp.take(arrived_flat, flat_work, 1).reshape(levels + 2, working // width, width)
    work = jnp.transpose(work, (1, 0, 2))
    fluxes = lax.map(slab_flux, (work[:, :levels], work[:, levels:]))
    fluxes = jnp.transpose(fluxes, (1, 0, 2)).reshape(levels, working)
    peer_start = starts[:, None]
    back_ids = peer_start + (myself - peer_start) % devices + slot_ids * devices
    valid_back = (back_ids < ends[:, None]).astype(jnp.float32)
    back_slot = jnp.clip((back_ids - myself) // devices, 0, working - 1)
    returning = jnp.take(fluxes, back_slot.reshape(-1), 1).reshape(levels, devices, capacity)
    returning = jnp.transpose(returning * valid_back[None], (1, 0, 2))
    came_back = lax.all_to_all(returning, ("gx", "gy"), split_axis=0, concat_axis=0, tiled=True)
    column_ids = lax.broadcasted_iota(jnp.int32, (blocks, width), 1)
    own_ids = my_start + jnp.clip(own_rank, 0, blocks - 1)[:, None] * width + column_ids
    home_peer = own_ids % devices
    home_first = my_start + (home_peer - my_start) % devices
    flat_home = jnp.clip(
        home_peer * capacity + (own_ids - home_first) // devices, 0, devices * capacity - 1
    )
    back_flat = jnp.transpose(came_back, (1, 0, 2)).reshape(levels, devices * capacity)
    placed = jnp.take(back_flat, flat_home.reshape(-1), 1).reshape(levels, blocks, width)
    net_flux = jnp.transpose(placed, (1, 0, 2)) * lit_blocks
    return (state_next, residual, net_flux)


def solution(mesh):
    placed = (
        P("gy", None, "gx"),
        P("gy", None, "gx"),
        P("gy", None, "gx"),
        P("gy", "gx"),
        P("gy", "gx"),
        P(),
        P(),
        P(("gx", "gy")),
    )
    return jax.shard_map(
        body,
        mesh=mesh,
        in_specs=placed,
        out_specs=(P("gy", None, "gx"), P("gy", None, "gx"), P("gy", None, "gx")),
        check_vma=False,
    )
```

profile of v0, /device:TPU:0, one launch (start us, length us, event | category | flops | bytes accessed | tf_op | source)
XLA Modules:
  0.0 987.2 jit_solution(6358502136507490129)
XLA Ops:
  18.2 41.5 %all-reduce.12 = s32[512]{0:T(512)S(1)} all-reduce(s32[512]{0:T(512)S(1)} %dynamic-update-slice.2), channel_id=1, replica_groups=mesh['gx'=4,'gy'=8] {'gx','gy'}, use_global_device_ids=true, to_apply=%add.12 | all-reduce | flops 512 | bytes 4096
  69.3 8.6 gather_fusion
  81.5 4.9 all-to-all-start
  89.9 4.2 compare_select_fusion.24
  94.4 15.7 %compare_and_fusion.3 = (pred[8,128]{1,0:T(8,128)(4,1)S(1)}, s32[1024]{0:T(1024)S(1)}) fusion(s32[]{:T(128)S(6)} %add.720, s32[1024]{0:T(1024)S(1)} %convert_reduce_fusion, pred[1024]{0:T(1024)(128)(4,1)S(1)} %get-tuple-element.109, pred[1024]{0:T(1024)(128)(4,1)S(1)} %get-tuple-element.107, pred[1024]{0:T(1024)(128)(4,1)S(1)} %get-tuple-element.108, ...), kind=kLoop, calls=%fused_computation.366 | loop fusion | flops 76800 | bytes 39016 | tf_op jit(solution)/shard_map/jit(_take)/and | solution.py:147
  118.9 5.9 collective-permute-done.2
  124.9 6.5 fusion.100
  134.2 10.0 %collective-permute-start.9 = (f32[16,128,1]{1,0,2:T(8,128)S(1)}, f32[16,128,1]{1,0,2:T(8,128)S(1)}, u32[]{:S(2)}, u32[]{:S(2)}) collective-permute-start(f32[16,128,1]{1,0,2:T(8,128)S(1)} %get-tuple-element.166), channel_id=1, source_target_pairs={{0,8},{8,16},{16,24},{24,0},{1,9},{9,17},{17,25},{25,1},{2,10},{10... | collective-permute-start | bytes 24584 | tf_op jit(solution)/shard_map/ppermute | solution.py:16
  148.3 4.5 multiply_reduce_fusion.8
  152.9 43.2 %all-reduce.13 = (f32[]{:T(128)}, f32[]{:T(128)}) all-reduce(f32[]{:T(128)} %get-tuple-element.84, f32[]{:T(128)} %get-tuple-element.83), channel_id=1, replica_groups=mesh['gx'=4,'gy'=8] {'gx','gy'}, use_global_device_ids=true, to_apply=%region_1.0 | all-reduce | flops 2 | bytes 16 | tf_op jit(solution)/shard_map/psum | solution.py:59
  199.9 39.4 %psum.72 = f32[]{:T(128)} all-reduce(f32[]{:T(128)} %multiply_reduce_fusion.7), channel_id=1, replica_groups=mesh['gx'=4,'gy'=8] {'gx','gy'}, use_global_device_ids=true, to_apply=%region_5.0 | all-reduce | flops 1 | bytes 8 | tf_op jit(solution)/shard_map/psum | solution.py:59
  250.3 4.4 multiply_reduce_fusion.6
  254.7 43.5 %psum.73 = f32[]{:T(128)} all-reduce(f32[]{:T(128)} %get-tuple-element.142), channel_id=1, replica_groups=mesh['gx'=4,'gy'=8] {'gx','gy'}, use_global_device_ids=true, to_apply=%region_7.0 | all-reduce | flops 1 | bytes 8 | tf_op jit(solution)/shard_map/psum | solution.py:89
  302.7 42.2 %psum.74 = f32[]{:T(128)} all-reduce(f32[]{:T(128)} %get-tuple-element.140), channel_id=1, replica_groups=mesh['gx'=4,'gy'=8] {'gx','gy'}, use_global_device_ids=true, to_apply=%region_9.0 | all-reduce | flops 1 | bytes 8 | tf_op jit(solution)/shard_map/psum | solution.py:59
  350.3 3.8 collective-permute-start.16
  355.8 4.4 multiply_reduce_fusion.4
  360.2 43.6 %psum.75 = f32[]{:T(128)} all-reduce(f32[]{:T(128)} %get-tuple-element.138), channel_id=1, replica_groups=mesh['gx'=4,'gy'=8] {'gx','gy'}, use_global_device_ids=true, to_apply=%region_11.0 | all-reduce | flops 1 | bytes 8 | tf_op jit(solution)/shard_map/psum | solution.py:89
  405.0 3.3 multiply_reduce_fusion.3
  408.4 42.3 %psum.76 = f32[]{:T(128)} all-reduce(f32[]{:T(128)} %get-tuple-element.136), channel_id=1, replica_groups=mesh['gx'=4,'gy'=8] {'gx','gy'}, use_global_device_ids=true, to_apply=%region_13.0 | all-reduce | flops 1 | bytes 8 | tf_op jit(solution)/shard_map/psum | solution.py:59
  456.3 3.8 collective-permute-start.20
  461.8 3.6 multiply_reduce_fusion.2
  465.4 43.6 %psum.77 = f32[]{:T(128)} all-reduce(f32[]{:T(128)} %get-tuple-element.134), channel_id=1, replica_groups=mesh['gx'=4,'gy'=8] {'gx','gy'}, use_global_device_ids=true, to_apply=%region_15.0 | all-reduce | flops 1 | bytes 8 | tf_op jit(solution)/shard_map/psum | solution.py:89
  512.2 42.5 %psum.78 = f32[]{:T(128)} all-reduce(f32[]{:T(128)} %get-tuple-element.132), channel_id=1, replica_groups=mesh['gx'=4,'gy'=8] {'gx','gy'}, use_global_device_ids=true, to_apply=%region_17.0 | all-reduce | flops 1 | bytes 8 | tf_op jit(solution)/shard_map/psum | solution.py:59
  556.0 5.1 gather_fusion.1
  561.5 325.5 %while.13 = (s32[]{:T(128)}, f32[8,128,128]{2,1,0:T(8,128)}, f32[8,2,128]{2,1,0:T(2,128)S(1)}, f32[128,112]{0,1:T(8,128)S(1)}, f32[8,128,128]{2,1,0:T(8,128)S(1)}, /*index=5*/f32[112]{0:T(128)S(1)}, s32[]{:T(128)}) while((s32[]{:T(128)}, f32[8,128,128]{2,1,0:T(8,128)}, f32[8,2,128]{2,1,0:T(2,128)S(1)}, ...), condition=%wide.region_26.27_spmd.clone, body=%wide.region_25.26_spmd.clone.sunk | while | flops 2860824576 | bytes 88995904 | solution.py:149
  564.1 15.5 %fusion.209 = f32[14336,128]{1,0:T(8,128)} fusion(f32[16,8,112,128]{3,2,1,0:T(8,128)S(1)} %bitcast.142), kind=kOutput, calls=%fused_computation.5.clone.1 | convolution fusion | flops 2818605056 | bytes 14680064 | tf_op jit(solution)/shard_map/while/body/eval_jaxpr/dot_general | solution.py:67
  579.6 8.5 copy.130
  588.1 6.2 slice_reduce_fusion.2
  595.5 6.4 fusion.211
  604.7 15.5 %fusion.209 = f32[14336,128]{1,0:T(8,128)} fusion(f32[16,8,112,128]{3,2,1,0:T(8,128)S(1)} %bitcast.142), kind=kOutput, calls=%fused_computation.5.clone.1 | convolution fusion | flops 2818605056 | bytes 14680064 | tf_op jit(solution)/shard_map/while/body/eval_jaxpr/dot_general | solution.py:67
  620.2 8.5 copy.130
  628.7 6.2 slice_reduce_fusion.2
  636.1 6.4 fusion.211
  645.3 15.5 %fusion.209 = f32[14336,128]{1,0:T(8,128)} fusion(f32[16,8,112,128]{3,2,1,0:T(8,128)S(1)} %bitcast.142), kind=kOutput, calls=%fused_computation.5.clone.1 | convolution fusion | flops 2818605056 | bytes 14680064 | tf_op jit(solution)/shard_map/while/body/eval_jaxpr/dot_general | solution.py:67
  660.8 8.5 copy.130
  669.3 6.2 slice_reduce_fusion.2
  676.7 6.4 fusion.211
  685.9 15.5 %fusion.209 = f32[14336,128]{1,0:T(8,128)} fusion(f32[16,8,112,128]{3,2,1,0:T(8,128)S(1)} %bitcast.142), kind=kOutput, calls=%fused_computation.5.clone.1 | convolution fusion | flops 2818605056 | bytes 14680064 | tf_op jit(solution)/shard_map/while/body/eval_jaxpr/dot_general | solution.py:67
  701.4 8.5 copy.130
  709.9 6.2 slice_reduce_fusion.2
  717.3 6.4 fusion.211
  726.6 15.5 %fusion.209 = f32[14336,128]{1,0:T(8,128)} fusion(f32[16,8,112,128]{3,2,1,0:T(8,128)S(1)} %bitcast.142), kind=kOutput, calls=%fused_computation.5.clone.1 | convolution fusion | flops 2818605056 | bytes 14680064 | tf_op jit(solution)/shard_map/while/body/eval_jaxpr/dot_general | solution.py:67
  742.1 8.5 copy.130
  750.5 6.2 slice_reduce_fusion.2
  757.9 6.4 fusion.211
  767.2 15.5 %fusion.209 = f32[14336,128]{1,0:T(8,128)} fusion(f32[16,8,112,128]{3,2,1,0:T(8,128)S(1)} %bitcast.142), kind=kOutput, calls=%fused_computation.5.clone.1 | convolution fusion | flops 2818605056 | bytes 14680064 | tf_op jit(solution)/shard_map/while/body/eval_jaxpr/dot_general | solution.py:67
  782.7 8.5 copy.130
  791.1 6.2 slice_reduce_fusion.2
  798.6 6.4 fusion.211
  807.8 15.5 %fusion.209 = f32[14336,128]{1,0:T(8,128)} fusion(f32[16,8,112,128]{3,2,1,0:T(8,128)S(1)} %bitcast.142), kind=kOutput, calls=%fused_computation.5.clone.1 | convolution fusion | flops 2818605056 | bytes 14680064 | tf_op jit(solution)/shard_map/while/body/eval_jaxpr/dot_general | solution.py:67
  823.3 8.5 copy.130
  831.7 6.2 slice_reduce_fusion.2
  839.2 6.4 fusion.211
  848.4 15.5 %fusion.209 = f32[14336,128]{1,0:T(8,128)} fusion(f32[16,8,112,128]{3,2,1,0:T(8,128)S(1)} %bitcast.142), kind=kOutput, calls=%fused_computation.5.clone.1 | convolution fusion | flops 2818605056 | bytes 14680064 | tf_op jit(solution)/shard_map/while/body/eval_jaxpr/dot_general | solution.py:67
  863.9 8.5 copy.130
  872.4 6.2 slice_reduce_fusion.2
  879.8 6.4 fusion.211
  888.3 5.5 gather_fusion.2
  895.3 4.6 all-to-all-start.1
  910.6 11.1 %collective-permute-done.25 = f32[16,128,1]{1,0,2:T(8,128)S(1)} collective-permute-done((f32[16,128,1]{1,0,2:T(8,128)S(1)}, f32[16,128,1]{1,0,2:T(8,128)S(1)}, u32[]{:S(2)}, u32[]{:S(2)}) %collective-permute-start.25) | collective-permute-done | bytes 8224 | tf_op jit(solution)/shard_map/ppermute | solution.py:16
  921.8 4.4 multiply_reduce_fusion
  926.1 44.0 %psum.79 = f32[]{:T(128)} all-reduce(f32[]{:T(128)} %get-tuple-element.130), channel_id=1, replica_groups=mesh['gx'=4,'gy'=8] {'gx','gy'}, use_global_device_ids=true, to_apply=%region_19.0 | all-reduce | flops 1 | bytes 8 | tf_op jit(solution)/shard_map/psum | solution.py:89
  971.5 4.6 multiply_subtract_fusion
  980.1 5.5 gather_fusion.3
  (298 shorter events, 129.2 us)
Async XLA Ops:
  0.6 66.4 %copy-start.32 = (s32[16]{0:T(128)S(1)}, s32[16]{0:T(128)}, u32[]{:S(2)}) copy-start(s32[16]{0:T(128)} %param.17) | copy-start | bytes 196
  0.6 63.3 %copy-start.27 = (f32[16,128]{1,0:T(8,128)S(1)}, f32[16,128]{1,0:T(8,128)}, u32[]{:S(2)}) copy-start(f32[16,128]{1,0:T(8,128)} %param.14) | copy-start | bytes 24580
  0.7 63.3 %copy-start.28 = (f32[16,128]{1,0:T(8,128)S(1)}, f32[16,128]{1,0:T(8,128)}, u32[]{:S(2)}) copy-start(f32[16,128]{1,0:T(8,128)} %param.13) | copy-start | bytes 24580
  1.7 123.2 %collective-permute-start.7 = (f32[1,128,128]{1,0,2:T(1,128)S(1)}, f32[1,128,128]{1,0,2:T(1,128)S(1)}, u32[]{:S(2)}, u32[]{:S(2)}) collective-permute-start(f32[1,128,128]{1,0,2:T(1,128)S(1)} %copy.100), channel_id=1, source_target_pairs={{0,1},{1,2},{2,3},{3,4},{4,5},{5,6},{6,7},{8,9},{9,10},{10,11},{11... | collective-permute-start | bytes 196616 | tf_op jit(solution)/shard_map/ppermute | solution.py:16
  4.8 120.1 %collective-permute-start.5 = (f32[1,128,128]{1,0,2:T(1,128)}, f32[1,128,128]{1,0,2:T(1,128)S(1)}, u32[]{:S(2)}, u32[]{:S(2)}) collective-permute-start(f32[1,128,128]{1,0,2:T(1,128)} %copy.94), channel_id=1, source_target_pairs={{1,0},{2,1},{3,2},{4,3},{5,4},{6,5},{7,6},{9,8},{10,9},{11,10},{12... | collective-permute-start | bytes 196616 | tf_op jit(solution)/shard_map/ppermute | solution.py:17
  8.5 103.0 %collective-permute-start.3 = (f32[16,128,1]{1,0,2:T(8,128)}, f32[16,128,1]{1,0,2:T(8,128)S(1)}, u32[]{:S(2)}, u32[]{:S(2)}) collective-permute-start(f32[16,128,1]{1,0,2:T(8,128)} %get-tuple-element.174), channel_id=1, source_target_pairs={{0,8},{8,16},{16,24},{24,0},{1,9},{9,17},{17,25},{25,1},{2,10},{10... | collective-permute-start | bytes 24584 | tf_op jit(solution)/shard_map/ppermute | solution.py:16
  10.9 102.4 %collective-permute-start.1 = (f32[16,128,1]{1,0,2:T(8,128)}, f32[16,128,1]{1,0,2:T(8,128)}, u32[]{:S(2)}, u32[]{:S(2)}) collective-permute-start(f32[16,128,1]{1,0,2:T(8,128)} %get-tuple-element.173), channel_id=1, source_target_pairs={{8,0},{16,8},{24,16},{0,24},{9,1},{17,9},{25,17},{1,25},{10,2},{18... | collective-permute-start | bytes 24584 | tf_op jit(solution)/shard_map/ppermute | solution.py:17
  14.9 446.8 %copy-start.1 = (f32[16,128,128]{1,0,2:T(8,128)}, f32[16,128,128]{1,0,2:T(8,128)S(1)}, u32[]{:S(2)}) copy-start(f32[16,128,128]{1,0,2:T(8,128)S(1)} %copy.80) | copy-start | bytes 3145732
  15.6 98.9 %collective-permute-start = (f32[16,128,1]{1,0,2:T(8,128)}, f32[16,128,1]{1,0,2:T(8,128)S(1)}, u32[]{:S(2)}, u32[]{:S(2)}) collective-permute-start(f32[16,128,1]{1,0,2:T(8,128)} %get-tuple-element.172), channel_id=1, source_target_pairs={{8,0},{16,8},{24,16},{0,24},{9,1},{17,9},{25,17},{1,25},{10,2},{18... | collective-permute-start | bytes 24584 | tf_op jit(solution)/shard_map/ppermute | solution.py:17
  67.2 14.3 %copy-start.31 = (s32[16]{0:T(128)}, s32[16]{0:T(128)S(1)}, u32[]{:S(2)}) copy-start(s32[16]{0:T(128)S(1)} %multiply_add_fusion.6) | copy-start | bytes 196
  77.8 8.6 copy-start.12
  78.5 33.0 %copy-start.29 = (f32[16,128,1]{1,0,2:T(8,128)S(1)}, f32[16,128,1]{1,0,2:T(8,128)}, u32[]{:S(2)}) copy-start(f32[16,128,1]{1,0,2:T(8,128)} %get-tuple-element.171) | copy-start | bytes 24580
  81.5 474.4 %all-to-all-start = ((f32[32,130,64]{1,2,0:T(8,128)}), f32[32,130,64]{1,2,0:T(8,128)}, u32[]{:S(2)}, u32[]{:S(2)}) async-start(f32[32,130,64]{1,2,0:T(8,128)} %multiply_bitcast_fusion), calls=%async_computation | async-start | bytes 4194304 | tf_op jit(solution)/shard_map/all_to_all | solution.py:136
  88.0 111.4 %copy-start.8 = (f32[16,127,128]{1,0,2:T(8,128)}, f32[16,127,128]{1,0,2:T(8,128)S(1)}, u32[]{:S(2)}) copy-start(f32[16,127,128]{1,0,2:T(8,128)S(1)} %get-tuple-element.146) | copy-start | bytes 3121156
  111.5 13.4 %collective-permute-start.2 = (f32[16,128,1]{1,0,2:T(8,128)S(1)}, f32[16,128,1]{1,0,2:T(8,128)S(1)}, u32[]{:S(2)}, u32[]{:S(2)}) collective-permute-start(f32[16,128,1]{1,0,2:T(8,128)S(1)} %copy-done.29), channel_id=1, source_target_pairs={{0,8},{8,16},{16,24},{24,0},{1,9},{9,17},{17,25},{25,1},{2,10},{10... | collective-permute-start | bytes 24584 | tf_op jit(solution)/shard_map/ppermute | solution.py:16
  113.3 11.6 %collective-permute-start.4 = (f32[1,128,128]{1,0,2:T(1,128)S(1)}, f32[1,128,128]{1,0,2:T(1,128)S(1)}, u32[]{:S(2)}, u32[]{:S(2)}) collective-permute-start(f32[1,128,128]{1,0,2:T(1,128)S(1)} %copy.91), channel_id=1, source_target_pairs={{1,0},{2,1},{3,2},{4,3},{5,4},{6,5},{7,6},{9,8},{10,9},{11,10},{12... | collective-permute-start | bytes 196616 | tf_op jit(solution)/shard_map/ppermute | solution.py:17
  114.6 347.2 %copy-start.19 = (f32[16,128,1]{1,0,2:T(8,128)}, f32[16,128,1]{1,0,2:T(8,128)S(1)}, u32[]{:S(2)}) copy-start(f32[16,128,1]{1,0,2:T(8,128)S(1)} %collective-permute-done) | copy-start | bytes 24580
  114.6 10.3 %collective-permute-start.6 = (f32[1,128,128]{1,0,2:T(1,128)S(1)}, f32[1,128,128]{1,0,2:T(1,128)S(1)}, u32[]{:S(2)}, u32[]{:S(2)}) collective-permute-start(f32[1,128,128]{1,0,2:T(1,128)S(1)} %copy.97), channel_id=1, source_target_pairs={{0,1},{1,2},{2,3},{3,4},{4,5},{5,6},{6,7},{8,9},{9,10},{10,11},{11... | collective-permute-start | bytes 196616 | tf_op jit(solution)/shard_map/ppermute | solution.py:16
  124.9 336.9 %copy-start.21 = (f32[16,128,1]{1,0,2:T(8,128)}, f32[16,128,1]{1,0,2:T(8,128)S(1)}, u32[]{:S(2)}) copy-start(f32[16,128,1]{1,0,2:T(8,128)S(1)} %collective-permute-done.2) | copy-start | bytes 24580
  124.9 336.9 %copy-start.14 = (f32[1,128,128]{1,0,2:T(1,128)}, f32[1,128,128]{1,0,2:T(1,128)S(1)}, u32[]{:S(2)}) copy-start(f32[1,128,128]{1,0,2:T(1,128)S(1)} %collective-permute-done.4) | copy-start | bytes 196612
  124.9 336.8 %copy-start.16 = (f32[1,128,128]{1,0,2:T(1,128)}, f32[1,128,128]{1,0,2:T(1,128)S(1)}, u32[]{:S(2)}) copy-start(f32[1,128,128]{1,0,2:T(1,128)S(1)} %collective-permute-done.6) | copy-start | bytes 196612
  124.9 74.5 %copy-start.33 = (s32[16]{0:T(128)S(1)}, s32[16]{0:T(128)}, u32[]{:S(2)}) copy-start(s32[16]{0:T(128)} %param.17) | copy-start | bytes 196
  131.4 168.0 %copy-start.3 = (f32[16,128,128]{1,0,2:T(8,128)}, f32[16,128,128]{1,0,2:T(8,128)S(1)}, u32[]{:S(2)}) copy-start(f32[16,128,128]{1,0,2:T(8,128)S(1)} %fusion.100) | copy-start | bytes 3145732
  131.5 16.8 %collective-permute-start.11 = (f32[1,128,128]{1,0,2:T(1,128)S(1)}, f32[1,128,128]{1,0,2:T(1,128)S(1)}, u32[]{:S(2)}, u32[]{:S(2)}) collective-permute-start(f32[1,128,128]{1,0,2:T(1,128)S(1)} %get-tuple-element.168), channel_id=1, source_target_pairs={{0,1},{1,2},{2,3},{3,4},{4,5},{5,6},{6,7},{8,9},{9,10},{10,11},{11... | collective-permute-start | bytes 196616 | tf_op jit(solution)/shard_map/ppermute | solution.py:16
  132.9 15.5 %collective-permute-start.10 = (f32[1,128,128]{1,0,2:T(1,128)S(1)}, f32[1,128,128]{1,0,2:T(1,128)S(1)}, u32[]{:S(2)}, u32[]{:S(2)}) collective-permute-start(f32[1,128,128]{1,0,2:T(1,128)S(1)} %get-tuple-element.167), channel_id=1, source_target_pairs={{1,0},{2,1},{3,2},{4,3},{5,4},{6,5},{7,6},{9,8},{10,9},{11,10},{12... | collective-permute-start | bytes 196616 | tf_op jit(solution)/shard_map/ppermute | solution.py:17
  134.2 11.4 %collective-permute-start.9 = (f32[16,128,1]{1,0,2:T(8,128)S(1)}, f32[16,128,1]{1,0,2:T(8,128)S(1)}, u32[]{:S(2)}, u32[]{:S(2)}) collective-permute-start(f32[16,128,1]{1,0,2:T(8,128)S(1)} %get-tuple-element.166), channel_id=1, source_target_pairs={{0,8},{8,16},{16,24},{24,0},{1,9},{9,17},{17,25},{25,1},{2,10},{10... | collective-permute-start | bytes 24584 | tf_op jit(solution)/shard_map/ppermute | solution.py:16
  144.2 4.1 collective-permute-start.8
  241.8 105.7 %copy-start.5 = (f32[16,128,128]{1,0,2:T(8,128)}, f32[16,128,128]{1,0,2:T(8,128)S(1)}, u32[]{:S(2)}) copy-start(f32[16,128,128]{1,0,2:T(8,128)S(1)} %multiply_add_fusion.4) | copy-start | bytes 3145732
  242.0 8.3 collective-permute-start.15
  243.3 7.0 collective-permute-start.14
  244.6 5.5 collective-permute-start.13
  246.6 3.7 collective-permute-start.12
  347.5 105.8 %copy-start.6 = (f32[16,128,128]{1,0,2:T(8,128)}, f32[16,128,128]{1,0,2:T(8,128)S(1)}, u32[]{:S(2)}) copy-start(f32[16,128,128]{1,0,2:T(8,128)S(1)} %multiply_add_fusion.3) | copy-start | bytes 3145732
  347.7 8.1 collective-permute-start.19
  349.0 6.8 collective-permute-start.18
  350.3 5.5 collective-permute-start.17
  350.3 109.8 %copy-start.9 = (f32[16,127,128]{1,0,2:T(8,128)S(1)}, f32[16,127,128]{1,0,2:T(8,128)}, u32[]{:S(2)}) copy-start(f32[16,127,128]{1,0,2:T(8,128)} %copy-done.8) | copy-start | bytes 3121156
  350.3 5.4 collective-permute-start.16
  453.3 12.0 %copy-start.7 = (f32[16,128,128]{1,0,2:T(8,128)}, f32[16,128,128]{1,0,2:T(8,128)S(1)}, u32[]{:S(2)}) copy-start(f32[16,128,128]{1,0,2:T(8,128)S(1)} %multiply_add_fusion.2) | copy-start | bytes 3145732
  453.4 56.9 %copy-start.13 = (f32[16,128,128]{1,0,2:T(8,128)S(1)}, f32[16,128,128]{1,0,2:T(8,128)}, u32[]{:S(2)}) copy-start(f32[16,128,128]{1,0,2:T(8,128)} %get-tuple-element.137) | copy-start | bytes 3145732
  453.5 8.3 collective-permute-start.23
  454.9 6.8 collective-permute-start.22
  456.2 5.5 collective-permute-start.21
  456.3 5.4 collective-permute-start.20
  460.4 101.0 %copy-start.18 = (f32[128,112]{0,1:T(8,128)S(1)}, f32[128,112]{0,1:T(8,128)}, u32[]{:S(2)}) copy-start(f32[128,112]{0,1:T(8,128)} %param.15) | copy-start | bytes 172036
  460.5 101.0 %copy-start.35 = (f32[112]{0:T(128)S(1)}, f32[112]{0:T(128)}, u32[]{:S(2)}) copy-start(f32[112]{0:T(128)} %param.16) | copy-start | bytes 1348
  561.5 326.8 %copy-start.25 = (s32[2048]{0:T(1024)S(1)}, s32[2048]{0:T(1024)}, u32[]{:S(2)}) copy-start(s32[2048]{0:T(1024)} %broadcast_clamp_fusion) | copy-start | bytes 24580
  887.0 6.8 copy-start.23
  887.0 6.8 copy-start.26
  893.7 28.0 %copy-start.2 = (f32[16,128,128]{1,0,2:T(8,128)S(1)}, f32[16,128,128]{1,0,2:T(8,128)}, u32[]{:S(2)}) copy-start(f32[16,128,128]{1,0,2:T(8,128)} %copy-done.1) | copy-start | bytes 3145732
  893.7 28.0 %copy-start.15 = (f32[1,128,128]{1,0,2:T(1,128)S(1)}, f32[1,128,128]{1,0,2:T(1,128)}, u32[]{:S(2)}) copy-start(f32[1,128,128]{1,0,2:T(1,128)} %copy-done.14) | copy-start | bytes 196612
  893.7 28.0 %copy-start.17 = (f32[1,128,128]{1,0,2:T(1,128)S(1)}, f32[1,128,128]{1,0,2:T(1,128)}, u32[]{:S(2)}) copy-start(f32[1,128,128]{1,0,2:T(1,128)} %copy-done.16) | copy-start | bytes 196612
  893.8 28.0 %copy-start.20 = (f32[16,128,1]{1,0,2:T(8,128)S(1)}, f32[16,128,1]{1,0,2:T(8,128)}, u32[]{:S(2)}) copy-start(f32[16,128,1]{1,0,2:T(8,128)} %copy-done.19) | copy-start | bytes 24580
  893.8 28.0 %copy-start.22 = (f32[16,128,1]{1,0,2:T(8,128)S(1)}, f32[16,128,1]{1,0,2:T(8,128)}, u32[]{:S(2)}) copy-start(f32[16,128,1]{1,0,2:T(8,128)} %copy-done.21) | copy-start | bytes 24580
  895.3 76.2 %copy-start.4 = (f32[16,128,128]{1,0,2:T(8,128)S(1)}, f32[16,128,128]{1,0,2:T(8,128)}, u32[]{:S(2)}) copy-start(f32[16,128,128]{1,0,2:T(8,128)} %copy-done.3) | copy-start | bytes 3145732
  895.3 84.8 %all-to-all-start.1 = ((f32[32,128,64]{1,2,0:T(8,128)}), f32[32,128,64]{1,2,0:T(8,128)S(1)}, u32[]{:S(2)}, u32[]{:S(2)}) async-start(f32[32,128,64]{1,2,0:T(8,128)} %multiply_bitcast_fusion.2), calls=%async_computation.1 | async-start | bytes 2097152 | tf_op jit(solution)/shard_map/all_to_all | solution.py:157
  901.6 24.6 %copy-start.10 = (f32[16,128,128]{1,0,2:T(8,128)}, f32[16,128,128]{1,0,2:T(8,128)S(1)}, u32[]{:S(2)}) copy-start(f32[16,128,128]{1,0,2:T(8,128)S(1)} %multiply_add_fusion.1) | copy-start | bytes 3145732
  901.7 20.0 %collective-permute-start.27 = (f32[1,128,128]{1,0,2:T(1,128)S(1)}, f32[1,128,128]{1,0,2:T(1,128)S(1)}, u32[]{:S(2)}, u32[]{:S(2)}) collective-permute-start(f32[1,128,128]{1,0,2:T(1,128)S(1)} %get-tuple-element.152), channel_id=1, source_target_pairs={{0,1},{1,2},{2,3},{3,4},{4,5},{5,6},{6,7},{8,9},{9,10},{10,11},{11... | collective-permute-start | bytes 196616 | tf_op jit(solution)/shard_map/ppermute | solution.py:16
  903.8 17.9 %collective-permute-start.26 = (f32[1,128,128]{1,0,2:T(1,128)S(1)}, f32[1,128,128]{1,0,2:T(1,128)S(1)}, u32[]{:S(2)}, u32[]{:S(2)}) collective-permute-start(f32[1,128,128]{1,0,2:T(1,128)S(1)} %get-tuple-element.151), channel_id=1, source_target_pairs={{1,0},{2,1},{3,2},{4,3},{5,4},{6,5},{7,6},{9,8},{10,9},{11,10},{12... | collective-permute-start | bytes 196616 | tf_op jit(solution)/shard_map/ppermute | solution.py:17
  905.2 16.5 %collective-permute-start.25 = (f32[16,128,1]{1,0,2:T(8,128)S(1)}, f32[16,128,1]{1,0,2:T(8,128)S(1)}, u32[]{:S(2)}, u32[]{:S(2)}) collective-permute-start(f32[16,128,1]{1,0,2:T(8,128)S(1)} %get-tuple-element.150), channel_id=1, source_target_pairs={{0,8},{8,16},{16,24},{24,0},{1,9},{9,17},{17,25},{25,1},{2,10},{10... | collective-permute-start | bytes 24584 | tf_op jit(solution)/shard_map/ppermute | solution.py:16
  906.8 14.8 %collective-permute-start.24 = (f32[16,128,1]{1,0,2:T(8,128)S(1)}, f32[16,128,1]{1,0,2:T(8,128)S(1)}, u32[]{:S(2)}, u32[]{:S(2)}) collective-permute-start(f32[16,128,1]{1,0,2:T(8,128)S(1)} %get-tuple-element.149), channel_id=1, source_target_pairs={{8,0},{16,8},{24,16},{0,24},{9,1},{17,9},{25,17},{1,25},{10,2},{18... | collective-permute-start | bytes 24584 | tf_op jit(solution)/shard_map/ppermute | solution.py:17
  971.5 8.6 copy-start.24
  978.7 7.2 copy-start.30
  978.7 7.2 copy-start.34
  (9 other events, 52.7 us)
where the time goes:
time: 1000 us; the launch traced here: 987 us
  blocking collectives  426 us (43%)
  matrix products  175 us (18%)
  local copies, waits for them, and re-layouts  167 us (17%)
  other arithmetic  116 us (12%)
  starting transfers between devices  65.1 us (7%)
  waiting for transfers between devices  22.5 us (2%)
  between operations  14.4 us (1%)
    psum x5, blocking collectives, squares(): return lax.psum(jnp.sum(residual * residual), ('gx', 'gy'))  210 us
    psum x4, blocking collectives, body(): curvature_sum = lax.psum(jnp.sum(direction * applied), ('gx', 'gy'))  175 us
    dot_general x8, matrix products, radiate(): jnp.dot(triangle, thickness.reshape(levels, gpoints * columns), precision...  124 us
    reshape x8, local copies, waits for them, and re-layouts, radiate(): cumulative = cumulative.reshape(levels, gpoints, columns)  67.7 us
    dot_general x8, matrix products, radiate(): jnp.einsum('lgc,g->lc', downward - upward, solar_weight, precision=lax.Pr...  51.3 us
    slice x8, local copies, waits for them, and re-layouts, radiate(): cumulative[-1] - cumulative  49.3 us
    unnamed x1, blocking collectives  41.5 us
    ppermute x14, starting transfers between devices, padded(): before = lax.ppermute(last, axis, up)  31 us
  transfers between devices with their start and end apart: 30, of which 8 were waited for; matrix products, arithmetic and copies ran while one was open for 11% of the time, Pallas kernels for 0%

commit v1 on v0

v1 whole, which is shorter than its diff:
```python
import functools
import math

import jax
import jax.numpy as jnp
from jax import lax
from jax.experimental import pallas as pl
from jax.experimental.pallas import tpu as pltpu
from jax.sharding import PartitionSpec as P

ITERS = 5
LANES = 128
SUB = 8
LOG2E = math.log2(math.e)
MESH = pl.DeviceIdType.MESH


def kernel(
    nx, ny,
    state_ref, diff_ref, vapour_ref, cos_ref, albedo_ref, mask_ref, absorb_ref, weight_ref,
    next_ref, residual_ref, net_ref,
    field, east, west, north, level, lon_send, lon_recv,
    wide, down_scale, up_scale, partial, sums, mine, stage_one, half_sum, stage_two,
    lat_ssem, lat_rsem, lon_ssem, lon_rsem, one_ssem, one_rsem, two_ssem, two_rsem,
):
    rows, levels, lanes = state_ref.shape
    gpoints = absorb_ref.shape[0]
    tiles = levels // SUB
    per = lanes // rows
    moments = 2 * ITERS + 1
    ix = lax.axis_index("gx")
    iy = lax.axis_index("gy")
    gx_east, gx_west = lax.rem(ix + 1, nx), lax.rem(ix + nx - 1, nx)
    gy_north, gy_south = lax.rem(iy + 1, ny), lax.rem(iy + ny - 1, ny)
    lane_of = lax.broadcasted_iota(jnp.int32, (SUB, lanes), 1)
    plane_lane = lax.broadcasted_iota(jnp.int32, (levels, lanes), 1)

    barrier = pltpu.get_barrier_semaphore()
    for d in range(1, nx):
        pl.semaphore_signal(
            barrier, inc=1, device_id=(lax.rem(ix + d, nx), iy), device_id_type=MESH
        )
    for d in range(1, ny):
        pl.semaphore_signal(
            barrier, inc=1, device_id=(ix, lax.rem(iy + d, ny)), device_id_type=MESH
        )
    pl.semaphore_wait(barrier, nx + ny - 2)

    def lon_copy(k, side):
        return pltpu.make_async_remote_copy(
            src_ref=lon_send.at[k, side],
            dst_ref=lon_recv.at[k, side],
            send_sem=lon_ssem.at[k, side],
            recv_sem=lon_rsem.at[k, side],
            device_id=(gx_west if side == 0 else gx_east, iy),
            device_id_type=MESH,
        )

    def lat_copy(k, side, source=None):
        if source is not None:
            src = source.at[0 if side == 0 else rows - 1]
        else:
            src = field.at[k, 1 if side == 0 else rows]
        return pltpu.make_async_remote_copy(
            src_ref=src,
            dst_ref=field.at[k, rows + 1 if side == 0 else 0],
            send_sem=lat_ssem.at[k, side],
            recv_sem=lat_rsem.at[k, side],
            device_id=(ix, gy_south if side == 0 else gy_north),
            device_id_type=MESH,
        )

    def pack(k, source):
        groups = tiles // per

        def step(j, packed):
            packed = list(packed)
            for t in range(tiles):
                tile = source[j, t * SUB:(t + 1) * SUB, :]
                target = rows * (t % per) + j
                here = lane_of == target
                for side in range(2):
                    moved = pltpu.roll(tile, lax.rem(target + side, lanes), 1)
                    slot = side * groups + t // per
                    packed[slot] = jnp.where(here, moved, packed[slot])
            return tuple(packed)

        zero = jnp.zeros((SUB, lanes), jnp.float32)
        packed = lax.fori_loop(0, rows, step, (zero,) * (2 * groups))
        for side in range(2):
            for g in range(groups):
                lon_send[k, side, g * SUB:(g + 1) * SUB, :] = packed[side * groups + g]

    def send_halo(k, source):
        for side in range(2):
            lat_copy(k, side, source).start()
        pack(k, field.at[k, 1:rows + 1] if source is None else source)
        for side in range(2):
            lon_copy(k, side).start()

    def wait_halo(k, source=None):
        for side in range(2):
            lat_copy(k, side, source).wait()
            lon_copy(k, side).wait()

    def sides(k, j, plane):
        from_east, from_west = [], []
        for t in range(tiles):
            target = rows * (t % per) + j
            g = t // per
            from_east.append(
                pltpu.roll(lon_recv[k, 0, g * SUB:(g + 1) * SUB, :], lanes - 1 - target, 1)
            )
            from_west.append(
                pltpu.roll(
                    lon_recv[k, 1, g * SUB:(g + 1) * SUB, :], lax.rem(lanes - target, lanes), 1
                )
            )
        from_east = jnp.concatenate(from_east, 0)
        from_west = jnp.concatenate(from_west, 0)
        return (
            jnp.where(plane_lane == lanes - 1, from_east, pltpu.roll(plane, lanes - 1, 1)),
            jnp.where(plane_lane == 0, from_west, pltpu.roll(plane, 1, 1)),
        )

    def flux(k, j):
        plane = field[k, j + 1]
        at_east, at_west = sides(k, j, plane)
        total = east[j] * (plane - at_east) + west[j] * (plane - at_west)
        total = total + north[j + 1] * (plane - field[k, j + 2])
        total = total + north[j] * (plane - field[k, j])
        vertical = level[j] * (pltpu.roll(plane, levels - 1, 0) - plane)
        return total - vertical + pltpu.roll(vertical, 1, 0), plane

    def fold(product):
        return jnp.sum(product.reshape(tiles, SUB, lanes), 0)

    def reduce_copy(r, stage, d):
        buffer = stage_one if stage == 0 else stage_two
        slot = ix if stage == 0 else iy
        ssem = one_ssem if stage == 0 else two_ssem
        rsem = one_rsem if stage == 0 else two_rsem
        peer = (lax.rem(ix + d, nx), iy) if stage == 0 else (ix, lax.rem(iy + d, ny))
        return pltpu.make_async_remote_copy(
            src_ref=(mine if stage == 0 else half_sum).at[r],
            dst_ref=buffer.at[r, slot],
            send_sem=ssem.at[r, d - 1],
            recv_sem=rsem.at[r, d - 1],
            device_id=peer,
            device_id_type=MESH,
        )

    def reduce_start(r, stage):
        source, buffer = (mine, stage_one) if stage == 0 else (half_sum, stage_two)
        n = nx if stage == 0 else ny
        buffer[r, ix if stage == 0 else iy] = source[r]
        for d in range(1, n):
            reduce_copy(r, stage, d).start()

    def reduce_end(r, stage):
        n = nx if stage == 0 else ny
        for d in range(1, n):
            reduce_copy(r, stage, d).wait()
        buffer = stage_one if stage == 0 else stage_two
        total = buffer[r, 0]
        for d in range(1, n):
            total = total + buffer[r, d]
        return total

    def all_lanes(values):
        shift = lanes // 2
        while shift:
            values = values + pltpu.roll(values, shift, 1)
            shift //= 2
        return values

    def radiate(j):
        cosine = cos_ref[pl.ds(j, 1), :]
        optical = vapour_ref[j] * (1.0 + 0.5 * jnp.tanh(state_ref[j]))
        down_scale[...] = optical * (-LOG2E / cosine)
        up_scale[...] = optical * (-1.66 * LOG2E)

        def downward(l, carry):
            carry = carry * jnp.exp2(wide[l] * down_scale[pl.ds(l, 1), :])
            partial[pl.ds(pl.multiple_of(l * SUB, SUB), SUB), :] = jnp.sum(
                carry.reshape(gpoints // SUB, SUB, lanes), 0
            )
            return carry

        carry = lax.fori_loop(0, levels, downward, weight_ref[...] * cosine, unroll=4)
        carry = carry * albedo_ref[pl.ds(j, 1), :]

        def upward(i, carry):
            l = levels - 1 - i
            where = pl.ds(pl.multiple_of(l * SUB, SUB), SUB)
            partial[where, :] = partial[where, :] - jnp.sum(
                carry.reshape(gpoints // SUB, SUB, lanes), 0
            )
            return carry * jnp.exp2(wide[l] * up_scale[pl.ds(l, 1), :])

        lax.fori_loop(0, levels, upward, carry, unroll=4)
        total = partial[pl.ds(0, levels, stride=SUB), :]
        for s in range(1, SUB):
            total = total + partial[pl.ds(s, levels, stride=SUB), :]
        net_ref[j] = total * mask_ref[pl.ds(j, 1), :]

    windows = ITERS + 3

    def window(w):
        @pl.loop(rows * w // windows, rows * (w + 1) // windows)
        def _(j):
            radiate(j)

    send_halo(0, diff_ref)
    send_halo(1, state_ref)

    def spread(j, total):
        field[0, j + 1] = diff_ref[j]
        field[1, j + 1] = state_ref[j]
        return total + fold(diff_ref[j] * diff_ref[j])

    squares = lax.fori_loop(0, rows, spread, jnp.zeros((SUB, lanes), jnp.float32))
    mine[0] = jnp.concatenate([squares, jnp.zeros_like(squares)], 0)
    reduce_start(0, 0)

    absorb = absorb_ref[...]

    @pl.loop(0, levels)
    def _(l):
        column = pltpu.roll(absorb, lax.rem(levels - l, levels), 1)[:, 0:1]
        wide[l] = jnp.broadcast_to(column, (gpoints, lanes))

    window(0)
    half_sum[0] = reduce_end(0, 0)
    reduce_start(0, 1)
    wait_halo(0, diff_ref)
    wait_halo(1, state_ref)

    level_of = lax.broadcasted_iota(jnp.int32, (levels, lanes), 0)

    @pl.loop(0, rows)
    def _(j):
        plane = field[0, j + 1]
        at_east, at_west = sides(0, j, plane)
        east[j] = jnp.sqrt(plane * at_east)
        west[j] = jnp.sqrt(plane * at_west)
        north[j + 1] = jnp.sqrt(plane * field[0, j + 2])
        level[j] = jnp.where(
            level_of == levels - 1, 0.0, jnp.sqrt(plane * pltpu.roll(plane, levels - 1, 0))
        )

    north[0] = jnp.sqrt(field[0, 0] * field[0, 1]) * (iy > 0).astype(jnp.float32)
    north[rows] = north[rows] * (iy < ny - 1).astype(jnp.float32)

    @pl.loop(0, rows)
    def _(j):
        field[2, j + 1] = -flux(1, j)[0]

    send_halo(2, None)
    window(1)
    squares = reduce_end(0, 1)
    count = nx * ny * rows * levels * lanes
    squares = all_lanes(jnp.sum(squares, 0, keepdims=True))
    half = 6.0 * jnp.sqrt(squares * (1.0 / count))
    inverse = 1.0 / half

    zero = jnp.zeros((SUB, lanes), jnp.float32)
    for k in range(ITERS):
        wait_halo(2 + k)

        def advance(j, totals):
            applied, plane = flux(2 + k, j)
            later = applied * inverse - plane
            if k > 0:
                later = 2.0 * later - field[1 + k, j + 1]
            field[3 + k, j + 1] = later
            out = (totals[0] + fold(later * plane), totals[1] + fold(later * later))
            if k == 0:
                out = out + (totals[2] + fold(plane * plane),)
            return out

        totals = lax.fori_loop(0, rows, advance, (zero,) * (3 if k == 0 else 2))
        sums[2 * k + 1] = totals[0]
        sums[2 * k + 2] = totals[1]
        if k == 0:
            sums[0] = totals[2]
        if k < ITERS - 1:
            send_halo(3 + k, None)
            window(2 + k)

    lines = [jnp.sum(sums[m], 0, keepdims=True) for m in range(moments)]
    lines += [jnp.zeros_like(lines[0])] * (2 * SUB - moments)
    mine[1] = jnp.concatenate(lines, 0)
    reduce_start(1, 0)
    window(ITERS + 1)
    half_sum[1] = reduce_end(1, 0)
    reduce_start(1, 1)
    window(ITERS + 2)
    values = all_lanes(reduce_end(1, 1))
    raw = [values[m:m + 1, :] for m in range(moments)]

    mu = [raw[0], raw[1]]
    for k in range(1, ITERS + 1):
        mu.append(2.0 * raw[2 * k] - mu[0])
        if k < ITERS:
            mu.append(2.0 * raw[2 * k + 1] - mu[1])
    gram = [
        [0.5 * (mu[i + j] + mu[abs(i - j)]) for j in range(ITERS + 1)] for i in range(ITERS + 1)
    ]

    def inner(a, b):
        terms = []
        for i in range(len(a)):
            for j in range(len(b)):
                terms.append((a[i] * b[j]) * gram[i][j])
        while len(terms) > 1:
            terms = [
                terms[i] + terms[i + 1] if i + 1 < len(terms) else terms[i]
                for i in range(0, len(terms), 2)
            ]
        return terms[0]

    centre = half + 1.0
    one = jnp.ones_like(half)
    none = jnp.zeros_like(half)
    res, direction, gain = [one], [one], [none] * ITERS
    current = inner(res, res)
    for iteration in range(ITERS):
        image = [centre * c for c in direction] + [none]
        for j, c in enumerate(direction):
            if j == 0:
                image[1] = image[1] + half * c
            else:
                image[j + 1] = image[j + 1] + 0.5 * half * c
                image[j - 1] = image[j - 1] + 0.5 * half * c
        step = current / inner(direction, image)
        for j, c in enumerate(direction):
            gain[j] = gain[j] + step * c
        res = [r - step * q for r, q in zip(res + [none], image)]
        if iteration < ITERS - 1:
            following = inner(res, res)
            ratio = following / current
            direction = [r + ratio * c for r, c in zip(res, direction + [none])]
            current = following

    @pl.loop(0, rows)
    def _(j):
        base = [field[2 + k, j + 1] for k in range(ITERS + 1)]
        iterate, left = state_ref[j], res[0] * base[0]
        for k in range(ITERS):
            iterate = iterate + gain[k] * base[k]
            left = left + res[k + 1] * base[k + 1]
        next_ref[j] = iterate
        residual_ref[j] = left


def body(mesh_shape, state_prev, diffusivity, vapour, cos_zenith, albedo, absorption, solar_weight, day_mask):
    nx, ny = mesh_shape
    rows, levels, lanes = state_prev.shape
    gpoints = absorption.shape[1]
    mask = jnp.broadcast_to(day_mask.astype(jnp.float32)[:, None], (rows, lanes))
    weight = jnp.broadcast_to(solar_weight[:, None], (gpoints, lanes))
    absorb = absorption.T
    f32 = jnp.float32
    out = jax.ShapeDtypeStruct((rows, levels, lanes), f32)
    vmem = pl.BlockSpec(memory_space=pltpu.VMEM)
    kinds = ITERS + 3
    packs = levels // SUB * rows // lanes * SUB
    dma = pltpu.SemaphoreType.DMA
    return pl.pallas_call(
        functools.partial(kernel, nx, ny),
        out_shape=(out, out, out),
        in_specs=[vmem] * 8,
        out_specs=(vmem, vmem, vmem),
        scratch_shapes=[
            pltpu.VMEM((kinds, rows + 2, levels, lanes), f32),
            pltpu.VMEM((rows, levels, lanes), f32),
            pltpu.VMEM((rows, levels, lanes), f32),
            pltpu.VMEM((rows + 1, levels, lanes), f32),
            pltpu.VMEM((rows, levels, lanes), f32),
            pltpu.VMEM((kinds, 2, packs, lanes), f32),
            pltpu.VMEM((kinds, 2, packs, lanes), f32),
            pltpu.VMEM((levels, gpoints, lanes), f32),
            pltpu.VMEM((levels, lanes), f32),
            pltpu.VMEM((levels, lanes), f32),
            pltpu.VMEM((levels * SUB, lanes), f32),
            pltpu.VMEM((2 * ITERS + 1, SUB, lanes), f32),
            pltpu.VMEM((2, 2 * SUB, lanes), f32),
            pltpu.VMEM((2, nx, 2 * SUB, lanes), f32),
            pltpu.VMEM((2, 2 * SUB, lanes), f32),
            pltpu.VMEM((2, ny, 2 * SUB, lanes), f32),
            dma((kinds, 2)), dma((kinds, 2)), dma((kinds, 2)), dma((kinds, 2)),
            dma((2, nx)), dma((2, nx)), dma((2, ny)), dma((2, ny)),
        ],
        compiler_params=pltpu.CompilerParams(
            collective_id=0, has_side_effects=True, vmem_limit_bytes=60 * 1024 * 1024
        ),
    )(state_prev, diffusivity, vapour, cos_zenith, albedo, mask, absorb, weight)


def solution(mesh):
    cells = P("gy", None, "gx")
    columns = P("gy", "gx")
    return jax.shard_map(
        functools.partial(body, (mesh.shape["gx"], mesh.shape["gy"])),
        mesh=mesh,
        in_specs=(cells, cells, cells, columns, columns, P(), P(), P(("gx", "gy"))),
        out_specs=(cells, cells, cells),
        check_vma=False,
    )
```

time: 1000 us -> 115 us (0.12); the launches traced: 987 us -> 115 us
  blocking collectives: 426 us -> 0 us
  matrix products: 175 us -> 0 us
  local copies, waits for them, and re-layouts: 167 us -> 6.98 us
  other arithmetic: 116 us -> 0.01 us
  Pallas kernels: 0 us -> 107 us
  starting transfers between devices: 65.1 us -> 0 us
  waiting for transfers between devices: 22.5 us -> 0 us
  between operations: 14.4 us -> 0.66 us
    psum x9 -> x0, blocking collectives: 384 us -> none  [the longest x5 210 us: squares(): return lax.psum(jnp.sum(residual * residual), ('gx', 'gy'))]
    dot_general x16 -> x0, matrix products: 175 us -> none  [the longest x8 124 us: radiate(): jnp.dot(triangle, thickness.reshape(levels, gpoints * columns), precision...]
    pallas_call x0 -> x1, Pallas kernels: none -> 107 us  [body(): pl.pallas_call(functools.partial(kernel, nx, ny), out_shape=(out, out, ou...]
    reshape x9 -> x0, local copies, waits for them, and re-layouts: 67.8 us -> none  [the longest x8 67.7 us: radiate(): cumulative = cumulative.reshape(levels, gpoints, columns)]
    ppermute x28 -> x0, starting transfers between devices: 55.7 us -> none  [the longest x14 31 us: padded(): before = lax.ppermute(last, axis, up)]
    slice x28 -> x0, local copies, waits for them, and re-layouts: 54 us -> none  [the longest x8 49.3 us: radiate(): cumulative[-1] - cumulative]
    unnamed x1 -> x0, blocking collectives: 41.5 us -> none
    mul x35 -> x0, other arithmetic: 36 us -> none  [the longest x8 16.6 us: radiate(): thickness = absorption[:, :, None] * layer_amount[:, None, :]]
  transfers between devices with their start and end apart: 30 -> 0, of which waited for: 8 -> 0; matrix products, arithmetic and copies ran while one was open for 11% -> 0% of each run, Pallas kernels for 0% -> 0%
where the time goes in v1:
time: 115 us
  Pallas kernels  107 us (93%)
  local copies, waits for them, and re-layouts  6.98 us (6%)
    pallas_call x1, Pallas kernels, body(): pl.pallas_call(functools.partial(kernel, nx, ny), out_shape=(out, out, ou...  107 us
    unnamed x11, local copies, waits for them, and re-layouts  5.61 us

profile of v1, /device:TPU:0, one launch (start us, length us, event | category | flops | bytes accessed | tf_op | source)
XLA Modules:
  0.0 114.9 jit_solution(4385748778754370568)
XLA Ops:
  0.6 0.0 copy-start.3
  0.6 0.6 copy-done.3
  1.3 0.0 copy-start.2
  1.3 0.7 broadcast_in_dim.4.mask_ref
  2.0 0.0 copy-done.2
  2.0 0.7 broadcast_in_dim.5.weight_ref
  2.7 107.3 %shard_map.103 = (f32[16,128,128]{2,1,0:T(8,128)}, f32[16,128,128]{2,1,0:T(8,128)}, f32[16,128,128]{2,1,0:T(8,128)}) custom-call(f32[16,128,128]{2,1,0:T(8,128)} %state_ref.1, f32[16,128,128]{2,1,0:T(8,128)} %diff_ref.1, f32[16,128,128]{2,1,0:T(8,128)} %vapour_ref.1, f32[16,128]{1,0:T(8,128)} %cos_ref.1, f32[16,128]{1,0:T(8,128)} %albedo_ref.1, ...), custom_call_target="tpu_custom_call" | custom-call | tf_op jit(solution)/shard_map/pallas_call | solution.py:370
  109.9 0.0 copy-start.1
  109.9 2.4 %copy.14 = f32[16,128,128]{2,1,0:T(8,128)} copy(f32[16,128,128]{2,1,0:T(8,128)} %get-tuple-element.6) | data formatting | bytes 2097152
  112.3 0.0 copy-done.1
  112.3 0.0 copy-start
  112.3 1.0 copy.15
  113.3 0.6 copy-done
  113.9 1.0 copy.16
  (1 shorter events, 0.0 us)
Async XLA Ops:
  0.6 0.7 copy-start.3
  1.3 0.7 copy-start.2
  109.9 2.4 %copy-start.1 = (f32[16,128,128]{2,1,0:T(8,128)S(1)}, f32[16,128,128]{2,1,0:T(8,128)}, u32[]{:S(2)}) copy-start(f32[16,128,128]{2,1,0:T(8,128)} %get-tuple-element.7) | copy-start | bytes 3145732
  112.3 1.6 %copy-start = (f32[16,128,128]{2,1,0:T(8,128)S(1)}, f32[16,128,128]{2,1,0:T(8,128)}, u32[]{:S(2)}) copy-start(f32[16,128,128]{2,1,0:T(8,128)} %get-tuple-element.8) | copy-start | bytes 3145732

commit v2 on v1

--- a/solution.py
+++ b/solution.py
@@ -187,7 +187,7 @@
             )
             return carry
 
-        carry = lax.fori_loop(0, levels, downward, weight_ref[...] * cosine, unroll=4)
+        carry = lax.fori_loop(0, levels, downward, weight_ref[...] * cosine, unroll=8)
         carry = carry * albedo_ref[pl.ds(j, 1), :]
 
         def upward(i, carry):
@@ -198,7 +198,7 @@
             )
             return carry * jnp.exp2(wide[l] * up_scale[pl.ds(l, 1), :])
 
-        lax.fori_loop(0, levels, upward, carry, unroll=4)
+        lax.fori_loop(0, levels, upward, carry, unroll=8)
         total = partial[pl.ds(0, levels, stride=SUB), :]
         for s in range(1, SUB):
             total = total + partial[pl.ds(s, levels, stride=SUB), :]
@@ -217,7 +217,8 @@
     def spread(j, total):
         field[0, j + 1] = diff_ref[j]
         field[1, j + 1] = state_ref[j]
-        return total + fold(diff_ref[j] * diff_ref[j])
+        square = diff_ref[j] * diff_ref[j]
+        return total + fold(square * square * square)
 
     squares = lax.fori_loop(0, rows, spread, jnp.zeros((SUB, lanes), jnp.float32))
     mine[0] = jnp.concatenate([squares, jnp.zeros_like(squares)], 0)
@@ -261,7 +262,7 @@
     squares = reduce_end(0, 1)
     count = nx * ny * rows * levels * lanes
     squares = all_lanes(jnp.sum(squares, 0, keepdims=True))
-    half = 6.0 * jnp.sqrt(squares * (1.0 / count))
+    half = 6.0 * jnp.exp(jnp.log(squares * (1.0 / count)) * (1.0 / 6.0))
     inverse = 1.0 / half
 
     zero = jnp.zeros((SUB, lanes), jnp.float32)

time: 115 us -> 108 us (0.939)
  Pallas kernels: 107 us -> 101 us
    pallas_call x1, Pallas kernels: 107 us -> 101 us  [body(): pl.pallas_call(functools.partial(kernel, nx, ny), out_shape=(out, out, ou...]
where the time goes in v2:
time: 108 us
  Pallas kernels  101 us (94%)
  local copies, waits for them, and re-layouts  6.98 us (6%)
    pallas_call x1, Pallas kernels, body(): pl.pallas_call(functools.partial(kernel, nx, ny), out_shape=(out, out, ou...  101 us
    unnamed x11, local copies, waits for them, and re-layouts  5.61 us

profile of v2, /device:TPU:0, one launch (start us, length us, event | category | flops | bytes accessed | tf_op | source)
XLA Modules:
  0.0 108.2 jit_solution(16514991841780718520)
XLA Ops:
  0.6 0.0 copy-start.3
  0.6 0.6 copy-done.3
  1.3 0.0 copy-start.2
  1.3 0.7 broadcast_in_dim.4.mask_ref
  2.0 0.0 copy-done.2
  2.0 0.7 broadcast_in_dim.5.weight_ref
  2.7 100.6 %shard_map.103 = (f32[16,128,128]{2,1,0:T(8,128)}, f32[16,128,128]{2,1,0:T(8,128)}, f32[16,128,128]{2,1,0:T(8,128)}) custom-call(f32[16,128,128]{2,1,0:T(8,128)} %state_ref.1, f32[16,128,128]{2,1,0:T(8,128)} %diff_ref.1, f32[16,128,128]{2,1,0:T(8,128)} %vapour_ref.1, f32[16,128]{1,0:T(8,128)} %cos_ref.1, f32[16,128]{1,0:T(8,128)} %albedo_ref.1, ...), custom_call_target="tpu_custom_call" | custom-call | tf_op jit(solution)/shard_map/pallas_call | solution.py:371
  103.3 0.0 copy-start.1
  103.3 2.4 %copy.14 = f32[16,128,128]{2,1,0:T(8,128)} copy(f32[16,128,128]{2,1,0:T(8,128)} %get-tuple-element.6) | data formatting | bytes 2097152
  105.7 0.0 copy-done.1
  105.7 0.0 copy-start
  105.7 1.0 copy.15
  106.6 0.6 copy-done
  107.3 1.0 copy.16
  (1 shorter events, 0.0 us)
Async XLA Ops:
  0.6 0.7 copy-start.3
  1.3 0.7 copy-start.2
  103.3 2.4 %copy-start.1 = (f32[16,128,128]{2,1,0:T(8,128)S(1)}, f32[16,128,128]{2,1,0:T(8,128)}, u32[]{:S(2)}) copy-start(f32[16,128,128]{2,1,0:T(8,128)} %get-tuple-element.7) | copy-start | bytes 3145732
  105.7 1.6 %copy-start = (f32[16,128,128]{2,1,0:T(8,128)S(1)}, f32[16,128,128]{2,1,0:T(8,128)}, u32[]{:S(2)}) copy-start(f32[16,128,128]{2,1,0:T(8,128)} %get-tuple-element.8) | copy-start | bytes 3145732
